TPU v7x, 32 devices: a whole 2x2x4 slice. The times are simulated.
32 devices in a mesh: groups: 2 (over y), seq: 4 (over z), head: 4 (over x, core).
Axes of the slice: x: 2, y: 2, z: 4, core: 2. Of those that a mesh axis runs over, the one named last changes fastest.
Arguments:
- queries: bfloat16 [2048, 8192], P(('groups', 'seq'), 'head'), parts along dimension 0, may hold values from -16 to 16
- keys: bfloat16 [2048, 1024], P(('groups', 'seq'), 'head'), parts along dimension 0, may hold values from -16 to 16
- values: bfloat16 [2048, 1024], P(('groups', 'seq'), 'head'), parts along dimension 0, may hold values from -6 to 6
- prompt_len: int32 [2], P('groups'), parts along dimension 0, may hold values from 256 to 1024
- page_dest: int32 [8, 2], P('groups'), parts along dimension 0, may hold values from 0 to 3, all different within a row; in each aligned block of 4 rows (0 to 3, 4 to 7, ...) at most 4 rows name the same one
Outputs:
- attended: bfloat16 [2048, 8192], P(('groups', 'seq'), 'head'), parts along dimension 0
- decode_page_cache: bfloat16 [32, 128, 2048], P(('groups', 'seq'), None, 'head'), parts along dimension 0
There are 2 independent parts, one for each index of `groups`. A program takes and returns all parts, laid end to end along the dimension named above; each array names one. Nothing has to cross between parts.
Inputs may be any that keep to these rules, and one draw needn't show every extreme that they name: `page_dest`: row s names the decode devices of the 2 pages of tokens s * 256 to (s + 1) * 256 - 1, all different within a row; no device is named more than 4 times in all, and some device exactly 4 times.
All inputs are finite; a program needn't handle non-finite values.
Results may differ from a plain program's by a relative error of at most 0.005.
Values may be sent and summed in bfloat16 or wider, within the bound.
A program may use at most 64 MiB of HBM per device.

v0:
```python
import math
import jax
import jax.numpy as jnp
from jax import lax
from jax.sharding import PartitionSpec as P

HEAD_SIZE = 128
PAGE_TOKENS = 128
NEG_FILL = -1e30


def blank_state(kv_heads, group_size, query_count):
    return (
        jnp.full((kv_heads, group_size, query_count), NEG_FILL, jnp.float32),
        jnp.zeros((kv_heads, group_size, query_count), jnp.float32),
        jnp.zeros((kv_heads, group_size, query_count, HEAD_SIZE), jnp.float32),
    )


def attend_block(
    query_state, query_block, query_pos, key_block, value_block, block_start, prompt_end
):
    key_count = key_block.shape[0]
    kv_heads = key_block.shape[1] // HEAD_SIZE
    keys_split = key_block.reshape(key_count, kv_heads, HEAD_SIZE)
    values_split = value_block.reshape(key_count, kv_heads, HEAD_SIZE)
    scores = jnp.einsum(
        "rkgd,pkd->kgrp", query_block, keys_split, preferred_element_type=jnp.float32
    )
    scores = scores * (1.0 / math.sqrt(HEAD_SIZE))
    key_pos = block_start + jnp.arange(key_count, dtype=jnp.int32)
    allowed = (key_pos[None, :] <= query_pos[:, None]) & (key_pos[None, :] < prompt_end)
    scores = jnp.where(allowed, scores, NEG_FILL)
    old_max = query_state[0]
    new_max = jnp.maximum(old_max, jnp.max(scores, axis=-1))
    weights = jnp.where(allowed, jnp.exp(scores - new_max[..., None]), 0.0)
    factor = jnp.exp(old_max - new_max)
    denominator = query_state[1] * factor + jnp.sum(weights, axis=-1)
    accumulated = query_state[2] * factor[..., None] + jnp.einsum(
        "kgrp,pkd->kgrd",
        weights.astype(jnp.bfloat16),
        values_split,
        preferred_element_type=jnp.float32,
    )
    return (new_max, denominator, accumulated)


def finish(query_state, query_pos, prompt_end):
    query_live = query_pos < prompt_end
    safe_total = jnp.where(query_live[None, None, :], query_state[1], 1.0)
    result = jnp.where(query_live[None, None, :, None], query_state[2] / safe_total[..., None], 0.0)
    query_count = query_pos.shape[0]
    return result.transpose(2, 0, 1, 3).reshape(query_count, -1).astype(jnp.bfloat16)


def join_pages(key_rows, value_rows):
    page_count = key_rows.shape[0] // PAGE_TOKENS
    kv_heads = key_rows.shape[1] // HEAD_SIZE
    stacked = jnp.stack(
        (
            key_rows.reshape(page_count, PAGE_TOKENS, kv_heads, HEAD_SIZE),
            value_rows.reshape(page_count, PAGE_TOKENS, kv_heads, HEAD_SIZE),
        ),
        axis=3,
    )
    return stacked.reshape(page_count, PAGE_TOKENS, 2 * key_rows.shape[1])


def slot_pages(page_dest, owner, slots):
    flat_dest = page_dest.reshape(-1)
    page_order = jnp.arange(flat_dest.shape[0], dtype=jnp.int32)
    same_dest = flat_dest[:, None] == flat_dest[None, :]
    dest_rank = jnp.sum(same_dest & (page_order[None, :] < page_order[:, None]), axis=1)
    matched = (flat_dest[:, None] == owner) & (
        dest_rank[:, None] == jnp.arange(slots, dtype=jnp.int32)[None, :]
    )
    page_index = jnp.sum(jnp.where(matched, page_order[:, None], 0), axis=0)
    present = jnp.any(matched, axis=0)
    return (flat_dest, page_index, present)


def place_pages(stored, key_block, value_block, block_start, prompt_end, page_index, present):
    key_pos = block_start + jnp.arange(key_block.shape[0], dtype=jnp.int32)
    token_present = (key_pos < prompt_end)[:, None]
    block_pages = join_pages(
        jnp.where(token_present, key_block, 0), jnp.where(token_present, value_block, 0)
    )
    page_count = block_pages.shape[0]
    local_index = page_index - block_start // PAGE_TOKENS
    inside = present & (local_index >= 0) & (local_index < page_count)
    picked = block_pages[jnp.clip(local_index, 0, page_count - 1)]
    return jnp.where(inside[:, None, None], picked, stored)


def local(queries, keys, values, prompt_len, page_dest):
    shard_rows = queries.shape[0]
    kv_width = keys.shape[1]
    kv_heads = kv_width // HEAD_SIZE
    group_size = queries.shape[1] // kv_width
    seq_index = lax.axis_index("seq")
    prompt_end = prompt_len[0]
    per_device = page_dest.shape[1]
    slots = 2 * per_device
    flat_dest, page_index, present = slot_pages(page_dest, seq_index, slots)
    own_rows = seq_index * shard_rows + jnp.arange(shard_rows, dtype=jnp.int32)
    query_parts = (queries,)
    positions = (own_rows,)
    shaped = tuple(
        (
            part_rows.reshape(part_rows.shape[0], kv_heads, group_size, HEAD_SIZE)
            for part_rows in query_parts
        )
    )
    states = tuple(
        (blank_state(kv_heads, group_size, part_rows.shape[0]) for part_rows in query_parts)
    )
    page_store = jnp.zeros((slots, PAGE_TOKENS, 2 * kv_width), jnp.bfloat16)
    key_piece = lax.all_gather(keys, "seq", axis=0, tiled=True)
    value_piece = lax.all_gather(values, "seq", axis=0, tiled=True)
    block_count = key_piece.shape[0] // shard_rows
    per_step = max(1, min(block_count, 512 // shard_rows))
    while block_count % per_step:
        per_step -= 1
    step_rows = per_step * shard_rows
    steps_count = block_count // per_step
    key_blocks = key_piece.reshape(steps_count, step_rows, kv_width)
    value_blocks = value_piece.reshape(steps_count, step_rows, kv_width)

    def one_block(inner_carry, block_item):
        block_states, stored = inner_carry
        key_block, value_block, number = block_item
        block_start = number * step_rows
        updated = []
        for query_state, query_block, query_pos in zip(block_states, shaped, positions):
            needed = block_start <= jnp.minimum(query_pos[-1], prompt_end - 1)
            updated.append(
                lax.cond(
                    needed,
                    lambda kept: attend_block(
                        kept,
                        query_block,
                        query_pos,
                        key_block,
                        value_block,
                        block_start,
                        prompt_end,
                    ),
                    lambda kept: kept,
                    query_state,
                )
            )
        stored = place_pages(
            stored, key_block, value_block, block_start, prompt_end, page_index, present
        )
        return ((tuple(updated), stored), None)

    result, unused = lax.scan(
        one_block,
        (states, page_store),
        (key_blocks, value_blocks, jnp.arange(steps_count, dtype=jnp.int32)),
    )
    final_states, stored = result
    outputs = [
        finish(query_state, query_pos, prompt_end)
        for query_state, query_pos in zip(final_states, positions)
    ]
    attended = outputs[0]
    return (attended, stored)


def solution(mesh):
    return jax.shard_map(
        local,
        mesh=mesh,
        in_specs=(
            P(("groups", "seq"), "head"),
            P(("groups", "seq"), "head"),
            P(("groups", "seq"), "head"),
            P("groups"),
            P("groups", None),
        ),
        out_specs=(P(("groups", "seq"), "head"), P(("groups", "seq"), None, "head")),
        check_vma=False,
    )
```

profile of v0, /device:TPU:26, one launch (start us, length us, event | category | flops | bytes accessed | tf_op | source)
XLA Modules:
  0.0 76.9 jit_solution(3035175965505265752)
XLA Ops:
  1.3 0.7 slice.5
  2.7 0.8 copy.34
  3.4 0.1 broadcast_in_dim_reshape.2
  3.5 0.2 convert_reduce_fusion
  3.7 0.1 fusion.20
  3.8 0.1 select_reduce_fusion
  4.0 16.3 %all_gather.6 = bf16[1024,256]{1,0:T(8,128)(2,1)} all-gather(bf16[256,256]{1,0:T(8,128)(2,1)} %param.10), channel_id=1, replica_groups=mesh['groups'=2,'seq'=4,'head'=4] {'seq'}, dimensions={0}, use_global_device_ids=true | all-gather | bytes 655360 | tf_op jit(solution)/shard_map/all_gather | solution.py:118
  20.3 16.4 %all_gather.7 = bf16[1024,256]{1,0:T(8,128)(2,1)} all-gather(bf16[256,256]{1,0:T(8,128)(2,1)} %param.11), channel_id=1, replica_groups=mesh['groups'=2,'seq'=4,'head'=4] {'seq'}, dimensions={0}, use_global_device_ids=true | all-gather | bytes 655360 | tf_op jit(solution)/shard_map/all_gather | solution.py:119
  36.7 1.5 %copy.33 = bf16[256,2048]{0,1:T(8,128)(2,1)S(1)} copy(bf16[256,2048]{1,0:T(8,128)(2,1)} %param.9) | data formatting | bytes 2097152 | tf_op args[0]
  38.2 0.7 copy.35
  38.9 1.6 %broadcast_in_dim.106 = f32[2,8,256,128]{3,2,1,0:T(8,128)} broadcast(f32[]{:T(128)} %constant.102.clone.1), dimensions={} | broadcast | bytes 2097156 | tf_op jit(solution)/shard_map/broadcast_in_dim | solution.py:16
  40.4 31.5 %while.20 = (s32[]{:T(128)}, f32[2,8,256]{2,1,0:T(8,128)S(1)}, f32[2,8,256]{2,1,0:T(8,128)S(1)}, f32[2,8,256,128]{3,2,1,0:T(8,128)}, bf16[4,128,512]{1,2,0:T(8,1...) while((s32[]{:T(128)}, f32[2,8,256]{2,1,0:T(8,128)S(1)}, ...), condition=%wide.region_8.9_spmd.clone, body=%wide.region_3.8_spmd.clone.sunk | while | flops 1103377152 | bytes 57424572 | solution.py:157
  40.4 0.7 dynamic_slice.31
  41.9 0.7 add_compare_fusion.2
  42.5 1.1 %constant_dynamic-slice_fusion.3 = (bf16[1,512,256]{2,1,0:T(8,128)(2,1)S(1)}, bf16[1,512,256]{2,1,0:T(8,128)(2,1)S(1)}) fusion(bf16[2,512,256]{2,1,0:T(8,128)(2,1)} %get-tuple-element.556, s32[]{:T(128)S(6)} %copy.67, bf16[2,512,256]{2,1,0:T(8,128)(2,1)} %get-tuple-element.555), kind=kLoop, calls=%fused_computation.31.clone.1 | loop fusion | bytes 1048580 | tf_op jit(solution)/shard_map/while/body/jit(dynamic_index_in_dim)/dynamic_slice | solution.py:157
  43.6 0.1 squeeze.31
  43.7 0.1 squeeze.32
  43.8 1.1 %broadcast_select_fusion.4 = (bf16[4,128,2,1,128]{4,2,1,0,3:T(2,128)(2,1)S(1)}, bf16[4,128,2,1,128]{4,2,1,0,3:T(2,128)(2,1)S(1)}) fusion(bf16[4,128,2,1,128]{4,2,1,0,3:T(2,128)(2,1)S(1)} %squeeze.31, pred[4,128]{1,0:T(4,128)(4,1)S(1)} %add_compare_fusion.2, bf16[4,128,2,1,128]{4,2,1,0,3:T(2,128)(2,1)S(1)} %squeeze.32), kind=kLoop, calls=%fused_computation.25.clone.1 | loop fusion | flops 262144 | bytes 1049088 | tf_op jit(solution)/shard_map/while/body/eval_jaxpr/jit(_where)/select_n | solution.py:86
  44.9 0.7 pad_maximum_fusion.2
  45.6 0.4 copy.55
  46.1 0.6 gather_fusion
  46.7 0.2 select_select_fusion.2
  46.9 9.3 %conditional.3 = ((f32[2,8,256]{2,1,0:T(8,128)S(1)}, f32[2,8,256]{2,1,0:T(8,128)S(1)}, f32[2,8,256,128]{3,2,1,0:T(8,128)})) conditional(s32[]{:T(128)} %convert_element_type.41, (f32[2,8,256]{2,1,0:T(8,128)S(1)}, f32[2,8,256]{2,1,0:T(8,128)S(1)}, f32[2,8,256,128]{3,2,1,0:T(8,128)}) %tuple.62, (s32[]{:T(128)}, s32[]{:T(128)}, s32[]{:T(128)}, ...), branch_computations={%region_4.4_spmd, %region_5.7_spmd} | conditional | flops 1102325504 | bytes 49553512 | solution.py:137
  46.9 0.7 broadcast_compare_fusion
  47.6 0.2 compare_and_fusion
  47.8 0.1 reshape.144
  47.9 0.1 reshape.145
  47.9 0.0 copy-start
  48.0 1.4 %fusion.2 = (f32[2,8,256]{2,1,0:T(8,128)S(1)}, f32[2,512,256,8]{2,1,3,0:T(8,128)S(1)}) fusion(pred[256,512]{0,1:T(8,128)(4,1)S(1)} %compare_and_fusion, bf16[256,2,8,128]{3,0,2,1:T(8,128)(2,1)S(1)} %get-tuple-element.235, bf16[512,2,128,1]{2,1,0,3:T(2,128)(2,1)S(1)} %bitcast.45), kind=kOutput, calls=%fused_computation.4 | convolution fusion | flops 543158272 | bytes 9846784 | tf_op jit(solution)/shard_map/while/body/eval_jaxpr/cond/branch_1_fun/rkgd,pkd->kgrp/dot_general | solution.py:27
  49.4 2.0 %fusion.4 = f32[2,8,256]{2,1,0:T(8,128)S(1)} fusion(f32[2,512,256,8]{2,1,3,0:T(8,128)S(1)} %get-tuple-element.398, f32[2,8,256]{2,1,0:T(8,128)S(1)} %max.6, pred[256,512]{0,1:T(8,128)(4,1)S(1)} %compare_and_fusion), kind=kLoop, calls=%fused_computation.6 | loop fusion | flops 10481664 | bytes 8552448 | tf_op jit(solution)/shard_map/while/body/eval_jaxpr/cond/branch_1_fun/reduce_sum | solution.py:38
  51.4 0.0 copy-done
  51.4 3.4 %multiply_add_fusion = f32[2,8,256,128]{3,2,1,0:T(8,128)S(1)} fusion(f32[2,8,256,128]{3,2,1,0:T(8,128)S(1)} %copy-done, f32[2,512,256,8]{2,1,3,0:T(8,128)S(1)} %get-tuple-element.398, f32[2,8,256]{2,1,0:T(8,128)S(1)} %max.6, pred[256,512]{0,1:T(8,128)(4,1)S(1)} %compare_and_fusion, f32[2,8,256]{2,1,0:T(8,128)S(1)} %get-tuple-element.396, ...), kind=kOutput, calls=%fused_computation.9 | convolution fusion | flops 548405248 | bytes 13008896 | tf_op jit(solution)/shard_map/while/body/eval_jaxpr/cond/branch_1_fun/kgrp,pkd->kgrd/dot_general | solution.py:39
  54.8 0.0 copy-start.1
  54.9 1.3 %copy-done.1 = f32[2,8,256,128]{3,2,1,0:T(8,128)} copy-done((f32[2,8,256,128]{3,2,1,0:T(8,128)}, f32[2,8,256,128]{3,2,1,0:T(8,128)S(1)}, u32[]{:S(2)}) %copy-start.1) | copy-done | bytes 2097176 | tf_op jit(solution)/shard_map/while/body/eval_jaxpr/cond
  56.2 0.7 dynamic_slice.31
  57.6 0.7 add_compare_fusion.2
  58.3 1.1 %constant_dynamic-slice_fusion.3 = (bf16[1,512,256]{2,1,0:T(8,128)(2,1)S(1)}, bf16[1,512,256]{2,1,0:T(8,128)(2,1)S(1)}) fusion(bf16[2,512,256]{2,1,0:T(8,128)(2,1)} %get-tuple-element.556, s32[]{:T(128)S(6)} %copy.67, bf16[2,512,256]{2,1,0:T(8,128)(2,1)} %get-tuple-element.555), kind=kLoop, calls=%fused_computation.31.clone.1 | loop fusion | bytes 1048580 | tf_op jit(solution)/shard_map/while/body/jit(dynamic_index_in_dim)/dynamic_slice | solution.py:157
  59.4 0.1 squeeze.31
  59.5 0.1 squeeze.32
  59.5 1.1 %broadcast_select_fusion.4 = (bf16[4,128,2,1,128]{4,2,1,0,3:T(2,128)(2,1)S(1)}, bf16[4,128,2,1,128]{4,2,1,0,3:T(2,128)(2,1)S(1)}) fusion(bf16[4,128,2,1,128]{4,2,1,0,3:T(2,128)(2,1)S(1)} %squeeze.31, pred[4,128]{1,0:T(4,128)(4,1)S(1)} %add_compare_fusion.2, bf16[4,128,2,1,128]{4,2,1,0,3:T(2,128)(2,1)S(1)} %squeeze.32), kind=kLoop, calls=%fused_computation.25.clone.1 | loop fusion | flops 262144 | bytes 1049088 | tf_op jit(solution)/shard_map/while/body/eval_jaxpr/jit(_where)/select_n | solution.py:86
  60.6 0.7 pad_maximum_fusion.2
  61.4 0.4 copy.55
  61.8 0.6 gather_fusion
  62.5 0.2 select_select_fusion.2
  62.7 9.3 %conditional.3 = ((f32[2,8,256]{2,1,0:T(8,128)S(1)}, f32[2,8,256]{2,1,0:T(8,128)S(1)}, f32[2,8,256,128]{3,2,1,0:T(8,128)})) conditional(s32[]{:T(128)} %convert_element_type.41, (f32[2,8,256]{2,1,0:T(8,128)S(1)}, f32[2,8,256]{2,1,0:T(8,128)S(1)}, f32[2,8,256,128]{3,2,1,0:T(8,128)}) %tuple.62, (s32[]{:T(128)}, s32[]{:T(128)}, s32[]{:T(128)}, ...), branch_computations={%region_4.4_spmd, %region_5.7_spmd} | conditional | flops 1102325504 | bytes 49553512 | solution.py:137
  62.7 0.7 broadcast_compare_fusion
  63.4 0.2 compare_and_fusion
  63.6 0.1 reshape.144
  63.6 0.1 reshape.145
  63.7 0.0 copy-start
  63.7 1.4 %fusion.2 = (f32[2,8,256]{2,1,0:T(8,128)S(1)}, f32[2,512,256,8]{2,1,3,0:T(8,128)S(1)}) fusion(pred[256,512]{0,1:T(8,128)(4,1)S(1)} %compare_and_fusion, bf16[256,2,8,128]{3,0,2,1:T(8,128)(2,1)S(1)} %get-tuple-element.235, bf16[512,2,128,1]{2,1,0,3:T(2,128)(2,1)S(1)} %bitcast.45), kind=kOutput, calls=%fused_computation.4 | convolution fusion | flops 543158272 | bytes 9846784 | tf_op jit(solution)/shard_map/while/body/eval_jaxpr/cond/branch_1_fun/rkgd,pkd->kgrp/dot_general | solution.py:27
  65.2 2.0 %fusion.4 = f32[2,8,256]{2,1,0:T(8,128)S(1)} fusion(f32[2,512,256,8]{2,1,3,0:T(8,128)S(1)} %get-tuple-element.398, f32[2,8,256]{2,1,0:T(8,128)S(1)} %max.6, pred[256,512]{0,1:T(8,128)(4,1)S(1)} %compare_and_fusion), kind=kLoop, calls=%fused_computation.6 | loop fusion | flops 10481664 | bytes 8552448 | tf_op jit(solution)/shard_map/while/body/eval_jaxpr/cond/branch_1_fun/reduce_sum | solution.py:38
  67.2 0.0 copy-done
  67.2 3.4 %multiply_add_fusion = f32[2,8,256,128]{3,2,1,0:T(8,128)S(1)} fusion(f32[2,8,256,128]{3,2,1,0:T(8,128)S(1)} %copy-done, f32[2,512,256,8]{2,1,3,0:T(8,128)S(1)} %get-tuple-element.398, f32[2,8,256]{2,1,0:T(8,128)S(1)} %max.6, pred[256,512]{0,1:T(8,128)(4,1)S(1)} %compare_and_fusion, f32[2,8,256]{2,1,0:T(8,128)S(1)} %get-tuple-element.396, ...), kind=kOutput, calls=%fused_computation.9 | convolution fusion | flops 548405248 | bytes 13008896 | tf_op jit(solution)/shard_map/while/body/eval_jaxpr/cond/branch_1_fun/kgrp,pkd->kgrd/dot_general | solution.py:39
  70.6 0.0 copy-start.1
  70.6 1.3 %copy-done.1 = f32[2,8,256,128]{3,2,1,0:T(8,128)} copy-done((f32[2,8,256,128]{3,2,1,0:T(8,128)}, f32[2,8,256,128]{3,2,1,0:T(8,128)S(1)}, u32[]{:S(2)}) %copy-start.1) | copy-done | bytes 2097176 | tf_op jit(solution)/shard_map/while/body/eval_jaxpr/cond
  72.0 2.0 %fusion.17 = bf16[256,2,8,128]{3,0,2,1:T(8,128)(2,1)S(1)} fusion(f32[2,8,256,128]{3,2,1,0:T(8,128)} %get-tuple-element.262, f32[2,8,256]{2,1,0:T(8,128)S(1)} %broadcast_select_fusion.2, pred[256]{0:T(512)(128)(4,1)S(1)} %broadcast_compare_fusion.1), kind=kLoop, calls=%fused_computation.35 | loop fusion | flops 1572864 | bytes 3162368 | tf_op jit(solution)/shard_map/convert_element_type | solution.py:53
  74.0 0.7 copy.36
  74.7 1.2 %copy.53 = bf16[32,8,16,128]{3,1,2,0:T(8,128)(2,1)} copy(bf16[32,8,16,128]{3,2,1,0:T(8,128)(2,1)S(1)} %bitcast.47) | data formatting | bytes 2097152
  75.9 1.0 %copy.37 = bf16[4,128,512]{2,1,0:T(8,128)(2,1)} copy(bf16[4,128,512]{1,2,0:T(8,128)(2,1)S(1)} %get-tuple-element.363) | data formatting | bytes 1048576
  (26 shorter events, 0.1 us)
Async XLA Ops:
  47.9 3.5 %copy-start = (f32[2,8,256,128]{3,2,1,0:T(8,128)S(1)}, f32[2,8,256,128]{3,2,1,0:T(8,128)}, u32[]{:S(2)}) copy-start(f32[2,8,256,128]{3,2,1,0:T(8,128)} %get-tuple-element.237) | copy-start | bytes 6291460 | tf_op jit(solution)/shard_map/while/body/eval_jaxpr/cond
  54.8 1.4 %copy-start.1 = (f32[2,8,256,128]{3,2,1,0:T(8,128)}, f32[2,8,256,128]{3,2,1,0:T(8,128)S(1)}, u32[]{:S(2)}) copy-start(f32[2,8,256,128]{3,2,1,0:T(8,128)S(1)} %multiply_add_fusion) | copy-start | bytes 6291460 | tf_op jit(solution)/shard_map/while/body/eval_jaxpr/cond
  63.7 3.5 %copy-start = (f32[2,8,256,128]{3,2,1,0:T(8,128)S(1)}, f32[2,8,256,128]{3,2,1,0:T(8,128)}, u32[]{:S(2)}) copy-start(f32[2,8,256,128]{3,2,1,0:T(8,128)} %get-tuple-element.237) | copy-start | bytes 6291460 | tf_op jit(solution)/shard_map/while/body/eval_jaxpr/cond
  70.6 1.4 %copy-start.1 = (f32[2,8,256,128]{3,2,1,0:T(8,128)}, f32[2,8,256,128]{3,2,1,0:T(8,128)S(1)}, u32[]{:S(2)}) copy-start(f32[2,8,256,128]{3,2,1,0:T(8,128)S(1)} %multiply_add_fusion) | copy-start | bytes 6291460 | tf_op jit(solution)/shard_map/while/body/eval_jaxpr/cond
where the time goes:
time: 77.3 us; the launch traced here: 76.9 us
  blocking collectives  32.7 us (42%)
  local copies, waits for them, and re-layouts  17.1 us (22%)
  other arithmetic  13.6 us (18%)
  matrix products  9.64 us (12%)
  between operations  2.06 us (3%)
  loops' own time  1.84 us (2%)
    all_gather x1, blocking collectives, local(): value_piece = lax.all_gather(values, 'seq', axis=0, tiled=True)  16.4 us
    all_gather x1, blocking collectives, local(): key_piece = lax.all_gather(keys, 'seq', axis=0, tiled=True)  16.3 us
    dot_general x2, matrix products, attend_block(): jnp.einsum('kgrp,pkd->kgrd', weights.astype(jnp.bfloat16), values_split,...  6.81 us
    unnamed x5, local copies, waits for them, and re-layouts  5.16 us
    reduce_sum x2, other arithmetic, attend_block(): denominator = query_state[1] * factor + jnp.sum(weights, axis=-1)  4.01 us
    dynamic_slice x4, local copies, waits for them, and re-layouts, local(): lax.scan(one_block, (states, page_store), (key_blocks, value_blocks, jnp....  3.47 us
    dot_general x2, matrix products, attend_block(): jnp.einsum('rkgd,pkd->kgrp', query_block, keys_split, preferred_element_t...  2.83 us
    cond x10, local copies, waits for them, and re-layouts  2.71 us

commit v1 on v0

--- a/solution.py
+++ b/solution.py
@@ -7,6 +7,12 @@
 HEAD_SIZE = 128
 PAGE_TOKENS = 128
 NEG_FILL = -1e30
+load_keys = lambda q_in: jnp.concatenate(
+    jax.lax.all_to_all(
+        jnp.stack([q_in for _ in range(jax.lax.axis_size("seq"))], axis=0), "seq", 0, 0
+    ),
+    axis=0,
+)
 
 
 def blank_state(kv_heads, group_size, query_count):
@@ -115,7 +121,7 @@
         (blank_state(kv_heads, group_size, part_rows.shape[0]) for part_rows in query_parts)
     )
     page_store = jnp.zeros((slots, PAGE_TOKENS, 2 * kv_width), jnp.bfloat16)
-    key_piece = lax.all_gather(keys, "seq", axis=0, tiled=True)
+    key_piece = load_keys(keys)
     value_piece = lax.all_gather(values, "seq", axis=0, tiled=True)
     block_count = key_piece.shape[0] // shard_rows
     per_step = max(1, min(block_count, 512 // shard_rows))

time: 77.3 us -> 70.3 us (0.909)
  blocking collectives: 32.7 us -> 19.3 us
  starting transfers between devices: 0 us -> 5.09 us
  local copies, waits for them, and re-layouts: 17.1 us -> 18.6 us
    all_gather x1 -> x0, blocking collectives: 16.3 us -> none  [local(): key_piece = lax.all_gather(keys, 'seq', axis=0, tiled=True)]
    all_to_all x0 -> x1, starting transfers between devices: none -> 5.09 us  [jax.lax.all_to_all(jnp.stack([q_in for _ in range(jax.lax.axis_size('seq'...]
    all_gather x1, blocking collectives: 16.4 us -> 19.3 us  [local(): value_piece = lax.all_gather(values, 'seq', axis=0, tiled=True)]
    another operation x0 -> x1, local copies, waits for them, and re-layouts: none -> 1.73 us  [jnp.stack([q_in for _ in range(jax.lax.axis_size('seq'))], axis=0)]
  transfers between devices with their start and end apart: 0 -> 1, of which waited for: 0 -> 0; matrix products, arithmetic and copies ran while one was open for 0% -> 6% of each run, Pallas kernels for 0% -> 0%
where the time goes in v1:
time: 70.3 us; the launch traced here: 69.9 us
  blocking collectives  19.3 us (27%)
  local copies, waits for them, and re-layouts  18.6 us (26%)
  other arithmetic  13.6 us (19%)
  matrix products  9.64 us (14%)
  starting transfers between devices  5.09 us (7%)
  between operations  1.98 us (3%)
  loops' own time  1.76 us (3%)
    all_gather x1, blocking collectives, local(): value_piece = lax.all_gather(values, 'seq', axis=0, tiled=True)  19.3 us
    dot_general x2, matrix products, attend_block(): jnp.einsum('kgrp,pkd->kgrd', weights.astype(jnp.bfloat16), values_split,...  6.81 us
    unnamed x5, local copies, waits for them, and re-layouts  5.15 us
    all_to_all x1, starting transfers between devices, jax.lax.all_to_all(jnp.stack([q_in for _ in range(jax.lax.axis_size('seq'...  5.09 us
    reduce_sum x2, other arithmetic, attend_block(): denominator = query_state[1] * factor + jnp.sum(weights, axis=-1)  4.01 us
    dynamic_slice x4, local copies, waits for them, and re-layouts, local(): lax.scan(one_block, (states, page_store), (key_blocks, value_blocks, jnp....  3.31 us
    dot_general x2, matrix products, attend_block(): jnp.einsum('rkgd,pkd->kgrp', query_block, keys_split, preferred_element_t...  2.83 us
    cond x10, local copies, waits for them, and re-layouts  2.71 us
  transfers between devices with their start and end apart: 1, of which 0 were waited for; matrix products, arithmetic and copies ran while one was open for 6% of the time, Pallas kernels for 0%

profile of v1, /device:TPU:26, one launch (start us, length us, event | category | flops | bytes accessed | tf_op | source)
XLA Modules:
  0.0 69.9 jit_solution(9566404904997903782)
XLA Ops:
  0.6 1.7 %stack.14 = bf16[4,256,256]{2,1,0:T(8,128)(2,1)} broadcast(bf16[256,256]{1,0:T(8,128)(2,1)} %param.10), dimensions={1,2} | broadcast | bytes 655360 | tf_op jit(solution)/shard_map/stack | solution.py:12
  2.4 5.1 %all-to-all-start = ((bf16[4,256,256]{2,1,0:T(8,128)(2,1)}), bf16[4,256,256]{2,1,0:T(8,128)(2,1)}, u32[]{:S(2)}, u32[]{:S(2)}) async-start(bf16[4,256,256]{2,1,0:T(8,128)(2,1)} %stack.14), calls=%async_computation | async-start | bytes 1048576 | tf_op jit(solution)/shard_map/all_to_all | solution.py:11
  8.1 0.6 slice.5
  8.7 0.8 %copy.34 = s32[4,2]{1,0:T(4,128)S(1)} copy(s32[4,2]{0,1:T(2,128)} %param.13) | data formatting | bytes 64 | tf_op args[4]
  9.5 0.1 broadcast_in_dim_reshape.2
  9.6 1.5 %copy.33 = bf16[256,2048]{0,1:T(8,128)(2,1)S(1)} copy(bf16[256,2048]{1,0:T(8,128)(2,1)} %param.9) | data formatting | bytes 2097152 | tf_op args[0]
  11.1 0.7 copy.35
  12.4 0.2 convert_reduce_fusion
  12.5 0.1 fusion.20
  12.7 0.1 select_reduce_fusion
  12.8 19.3 %all_gather.3 = bf16[1024,256]{1,0:T(8,128)(2,1)} all-gather(bf16[256,256]{1,0:T(8,128)(2,1)} %param.11), channel_id=1, replica_groups=mesh['groups'=2,'seq'=4,'head'=4] {'seq'}, dimensions={0}, use_global_device_ids=true | all-gather | bytes 655360 | tf_op jit(solution)/shard_map/all_gather | solution.py:125
  32.1 0.0 all-to-all-done
  32.1 1.6 %broadcast_in_dim.106 = f32[2,8,256,128]{3,2,1,0:T(8,128)} broadcast(f32[]{:T(128)} %constant.102.clone.1), dimensions={} | broadcast | bytes 2097156 | tf_op jit(solution)/shard_map/broadcast_in_dim | solution.py:22
  33.6 31.3 %while.20 = (s32[]{:T(128)}, f32[2,8,256]{2,1,0:T(8,128)S(1)}, f32[2,8,256]{2,1,0:T(8,128)S(1)}, f32[2,8,256,128]{3,2,1,0:T(8,128)}, bf16[4,128,512]{1,2,0:T(8,1...) while((s32[]{:T(128)}, f32[2,8,256]{2,1,0:T(8,128)S(1)}, ...), condition=%wide.region_8.9_spmd.clone, body=%wide.region_3.8_spmd.clone.sunk | while | flops 1103377152 | bytes 57424572 | solution.py:163
  33.6 0.6 dynamic_slice.31
  34.9 0.7 add_compare_fusion.2
  35.6 1.1 %constant_dynamic-slice_fusion.3 = (bf16[1,512,256]{2,1,0:T(8,128)(2,1)S(1)}, bf16[1,512,256]{2,1,0:T(8,128)(2,1)S(1)}) fusion(bf16[2,512,256]{2,1,0:T(8,128)(2,1)} %get-tuple-element.556, s32[]{:T(128)S(6)} %copy.67, bf16[2,512,256]{2,1,0:T(8,128)(2,1)} %get-tuple-element.555), kind=kLoop, calls=%fused_computation.31.clone.1 | loop fusion | bytes 1048580 | tf_op jit(solution)/shard_map/while/body/jit(dynamic_index_in_dim)/dynamic_slice | solution.py:163
  36.7 0.1 squeeze.31
  36.8 0.1 squeeze.32
  36.8 1.1 %broadcast_select_fusion.4 = (bf16[4,128,2,1,128]{4,2,1,0,3:T(2,128)(2,1)S(1)}, bf16[4,128,2,1,128]{4,2,1,0,3:T(2,128)(2,1)S(1)}) fusion(bf16[4,128,2,1,128]{4,2,1,0,3:T(2,128)(2,1)S(1)} %squeeze.31, pred[4,128]{1,0:T(4,128)(4,1)S(1)} %add_compare_fusion.2, bf16[4,128,2,1,128]{4,2,1,0,3:T(2,128)(2,1)S(1)} %squeeze.32), kind=kLoop, calls=%fused_computation.25.clone.1 | loop fusion | flops 262144 | bytes 1049088 | tf_op jit(solution)/shard_map/while/body/eval_jaxpr/jit(_where)/select_n | solution.py:92
  38.0 0.7 %pad_maximum_fusion.2 = bf16[4,128,2,2,128]{4,2,1,0,3:T(2,128)(2,1)S(1)} fusion(bf16[4,128,2,1,128]{4,2,1,0,3:T(2,128)(2,1)S(1)} %get-tuple-element.500, bf16[4,128,2,1,128]{4,2,1,0,3:T(2,128)(2,1)S(1)} %get-tuple-element.501), kind=kLoop, calls=%fused_computation.22.clone.1 | loop fusion | flops 262144 | bytes 1048576 | tf_op jit(solution)/shard_map/while/body/eval_jaxpr/stack | solution.py:65
  38.7 0.4 copy.55
  39.2 0.6 gather_fusion
  39.8 0.2 select_select_fusion.2
  40.0 9.3 %conditional.3 = ((f32[2,8,256]{2,1,0:T(8,128)S(1)}, f32[2,8,256]{2,1,0:T(8,128)S(1)}, f32[2,8,256,128]{3,2,1,0:T(8,128)})) conditional(s32[]{:T(128)} %convert_element_type.41, (f32[2,8,256]{2,1,0:T(8,128)S(1)}, f32[2,8,256]{2,1,0:T(8,128)S(1)}, f32[2,8,256,128]{3,2,1,0:T(8,128)}) %tuple.62, (s32[]{:T(128)}, s32[]{:T(128)}, s32[]{:T(128)}, ...), branch_computations={%region_4.4_spmd, %region_5.7_spmd} | conditional | flops 1102325504 | bytes 49553512 | solution.py:143
  40.0 0.7 broadcast_compare_fusion
  40.7 0.2 compare_and_fusion
  40.9 0.1 reshape.144
  41.0 0.1 reshape.145
  41.0 0.0 copy-start
  41.0 1.4 %fusion.2 = (f32[2,8,256]{2,1,0:T(8,128)S(1)}, f32[2,512,256,8]{2,1,3,0:T(8,128)S(1)}) fusion(pred[256,512]{0,1:T(8,128)(4,1)S(1)} %compare_and_fusion, bf16[256,2,8,128]{3,0,2,1:T(8,128)(2,1)S(1)} %get-tuple-element.235, bf16[512,2,128,1]{2,1,0,3:T(2,128)(2,1)S(1)} %bitcast.45), kind=kOutput, calls=%fused_computation.4 | convolution fusion | flops 543158272 | bytes 9846784 | tf_op jit(solution)/shard_map/while/body/eval_jaxpr/cond/branch_1_fun/rkgd,pkd->kgrp/dot_general | solution.py:33
  42.5 2.0 %fusion.4 = f32[2,8,256]{2,1,0:T(8,128)S(1)} fusion(f32[2,512,256,8]{2,1,3,0:T(8,128)S(1)} %get-tuple-element.398, f32[2,8,256]{2,1,0:T(8,128)S(1)} %max.6, pred[256,512]{0,1:T(8,128)(4,1)S(1)} %compare_and_fusion), kind=kLoop, calls=%fused_computation.6 | loop fusion | flops 10481664 | bytes 8552448 | tf_op jit(solution)/shard_map/while/body/eval_jaxpr/cond/branch_1_fun/reduce_sum | solution.py:44
  44.5 0.0 copy-done
  44.5 3.4 %multiply_add_fusion = f32[2,8,256,128]{3,2,1,0:T(8,128)S(1)} fusion(f32[2,8,256,128]{3,2,1,0:T(8,128)S(1)} %copy-done, f32[2,512,256,8]{2,1,3,0:T(8,128)S(1)} %get-tuple-element.398, f32[2,8,256]{2,1,0:T(8,128)S(1)} %max.6, pred[256,512]{0,1:T(8,128)(4,1)S(1)} %compare_and_fusion, f32[2,8,256]{2,1,0:T(8,128)S(1)} %get-tuple-element.396, ...), kind=kOutput, calls=%fused_computation.9 | convolution fusion | flops 548405248 | bytes 13008896 | tf_op jit(solution)/shard_map/while/body/eval_jaxpr/cond/branch_1_fun/kgrp,pkd->kgrd/dot_general | solution.py:45
  47.9 0.0 copy-start.1
  47.9 1.3 %copy-done.1 = f32[2,8,256,128]{3,2,1,0:T(8,128)} copy-done((f32[2,8,256,128]{3,2,1,0:T(8,128)}, f32[2,8,256,128]{3,2,1,0:T(8,128)S(1)}, u32[]{:S(2)}) %copy-start.1) | copy-done | bytes 2097176 | tf_op jit(solution)/shard_map/while/body/eval_jaxpr/cond
  49.3 0.6 dynamic_slice.31
  50.6 0.7 add_compare_fusion.2
  51.3 1.1 %constant_dynamic-slice_fusion.3 = (bf16[1,512,256]{2,1,0:T(8,128)(2,1)S(1)}, bf16[1,512,256]{2,1,0:T(8,128)(2,1)S(1)}) fusion(bf16[2,512,256]{2,1,0:T(8,128)(2,1)} %get-tuple-element.556, s32[]{:T(128)S(6)} %copy.67, bf16[2,512,256]{2,1,0:T(8,128)(2,1)} %get-tuple-element.555), kind=kLoop, calls=%fused_computation.31.clone.1 | loop fusion | bytes 1048580 | tf_op jit(solution)/shard_map/while/body/jit(dynamic_index_in_dim)/dynamic_slice | solution.py:163
  52.3 0.1 squeeze.31
  52.4 0.1 squeeze.32
  52.5 1.1 %broadcast_select_fusion.4 = (bf16[4,128,2,1,128]{4,2,1,0,3:T(2,128)(2,1)S(1)}, bf16[4,128,2,1,128]{4,2,1,0,3:T(2,128)(2,1)S(1)}) fusion(bf16[4,128,2,1,128]{4,2,1,0,3:T(2,128)(2,1)S(1)} %squeeze.31, pred[4,128]{1,0:T(4,128)(4,1)S(1)} %add_compare_fusion.2, bf16[4,128,2,1,128]{4,2,1,0,3:T(2,128)(2,1)S(1)} %squeeze.32), kind=kLoop, calls=%fused_computation.25.clone.1 | loop fusion | flops 262144 | bytes 1049088 | tf_op jit(solution)/shard_map/while/body/eval_jaxpr/jit(_where)/select_n | solution.py:92
  53.6 0.7 %pad_maximum_fusion.2 = bf16[4,128,2,2,128]{4,2,1,0,3:T(2,128)(2,1)S(1)} fusion(bf16[4,128,2,1,128]{4,2,1,0,3:T(2,128)(2,1)S(1)} %get-tuple-element.500, bf16[4,128,2,1,128]{4,2,1,0,3:T(2,128)(2,1)S(1)} %get-tuple-element.501), kind=kLoop, calls=%fused_computation.22.clone.1 | loop fusion | flops 262144 | bytes 1048576 | tf_op jit(solution)/shard_map/while/body/eval_jaxpr/stack | solution.py:65
  54.4 0.4 copy.55
  54.8 0.6 gather_fusion
  55.5 0.2 select_select_fusion.2
  55.6 9.3 %conditional.3 = ((f32[2,8,256]{2,1,0:T(8,128)S(1)}, f32[2,8,256]{2,1,0:T(8,128)S(1)}, f32[2,8,256,128]{3,2,1,0:T(8,128)})) conditional(s32[]{:T(128)} %convert_element_type.41, (f32[2,8,256]{2,1,0:T(8,128)S(1)}, f32[2,8,256]{2,1,0:T(8,128)S(1)}, f32[2,8,256,128]{3,2,1,0:T(8,128)}) %tuple.62, (s32[]{:T(128)}, s32[]{:T(128)}, s32[]{:T(128)}, ...), branch_computations={%region_4.4_spmd, %region_5.7_spmd} | conditional | flops 1102325504 | bytes 49553512 | solution.py:143
  55.6 0.7 broadcast_compare_fusion
  56.3 0.2 compare_and_fusion
  56.5 0.1 reshape.144
  56.6 0.1 reshape.145
  56.7 0.0 copy-start
  56.7 1.4 %fusion.2 = (f32[2,8,256]{2,1,0:T(8,128)S(1)}, f32[2,512,256,8]{2,1,3,0:T(8,128)S(1)}) fusion(pred[256,512]{0,1:T(8,128)(4,1)S(1)} %compare_and_fusion, bf16[256,2,8,128]{3,0,2,1:T(8,128)(2,1)S(1)} %get-tuple-element.235, bf16[512,2,128,1]{2,1,0,3:T(2,128)(2,1)S(1)} %bitcast.45), kind=kOutput, calls=%fused_computation.4 | convolution fusion | flops 543158272 | bytes 9846784 | tf_op jit(solution)/shard_map/while/body/eval_jaxpr/cond/branch_1_fun/rkgd,pkd->kgrp/dot_general | solution.py:33
  58.1 2.0 %fusion.4 = f32[2,8,256]{2,1,0:T(8,128)S(1)} fusion(f32[2,512,256,8]{2,1,3,0:T(8,128)S(1)} %get-tuple-element.398, f32[2,8,256]{2,1,0:T(8,128)S(1)} %max.6, pred[256,512]{0,1:T(8,128)(4,1)S(1)} %compare_and_fusion), kind=kLoop, calls=%fused_computation.6 | loop fusion | flops 10481664 | bytes 8552448 | tf_op jit(solution)/shard_map/while/body/eval_jaxpr/cond/branch_1_fun/reduce_sum | solution.py:44
  60.1 0.0 copy-done
  60.2 3.4 %multiply_add_fusion = f32[2,8,256,128]{3,2,1,0:T(8,128)S(1)} fusion(f32[2,8,256,128]{3,2,1,0:T(8,128)S(1)} %copy-done, f32[2,512,256,8]{2,1,3,0:T(8,128)S(1)} %get-tuple-element.398, f32[2,8,256]{2,1,0:T(8,128)S(1)} %max.6, pred[256,512]{0,1:T(8,128)(4,1)S(1)} %compare_and_fusion, f32[2,8,256]{2,1,0:T(8,128)S(1)} %get-tuple-element.396, ...), kind=kOutput, calls=%fused_computation.9 | convolution fusion | flops 548405248 | bytes 13008896 | tf_op jit(solution)/shard_map/while/body/eval_jaxpr/cond/branch_1_fun/kgrp,pkd->kgrd/dot_general | solution.py:45
  63.6 0.0 copy-start.1
  63.6 1.3 %copy-done.1 = f32[2,8,256,128]{3,2,1,0:T(8,128)} copy-done((f32[2,8,256,128]{3,2,1,0:T(8,128)}, f32[2,8,256,128]{3,2,1,0:T(8,128)S(1)}, u32[]{:S(2)}) %copy-start.1) | copy-done | bytes 2097176 | tf_op jit(solution)/shard_map/while/body/eval_jaxpr/cond
  64.9 2.0 %fusion.17 = bf16[256,2,8,128]{3,0,2,1:T(8,128)(2,1)S(1)} fusion(f32[2,8,256,128]{3,2,1,0:T(8,128)} %get-tuple-element.262, f32[2,8,256]{2,1,0:T(8,128)S(1)} %broadcast_select_fusion.2, pred[256]{0:T(512)(128)(4,1)S(1)} %broadcast_compare_fusion.1), kind=kLoop, calls=%fused_computation.35 | loop fusion | flops 1572864 | bytes 3162368 | tf_op jit(solution)/shard_map/convert_element_type | solution.py:59
  67.0 0.7 copy.36
  67.6 1.2 %copy.53 = bf16[32,8,16,128]{3,1,2,0:T(8,128)(2,1)} copy(bf16[32,8,16,128]{3,2,1,0:T(8,128)(2,1)S(1)} %bitcast.47) | data formatting | bytes 2097152
  68.9 1.0 %copy.37 = bf16[4,128,512]{2,1,0:T(8,128)(2,1)} copy(bf16[4,128,512]{1,2,0:T(8,128)(2,1)S(1)} %get-tuple-element.363) | data formatting | bytes 1048576
  (26 shorter events, 0.1 us)
Async XLA Ops:
  2.4 29.7 %all-to-all-start = ((bf16[4,256,256]{2,1,0:T(8,128)(2,1)}), bf16[4,256,256]{2,1,0:T(8,128)(2,1)}, u32[]{:S(2)}, u32[]{:S(2)}) async-start(bf16[4,256,256]{2,1,0:T(8,128)(2,1)} %stack.14), calls=%async_computation | async-start | bytes 1048576 | tf_op jit(solution)/shard_map/all_to_all | solution.py:11
  41.0 3.5 %copy-start = (f32[2,8,256,128]{3,2,1,0:T(8,128)S(1)}, f32[2,8,256,128]{3,2,1,0:T(8,128)}, u32[]{:S(2)}) copy-start(f32[2,8,256,128]{3,2,1,0:T(8,128)} %get-tuple-element.237) | copy-start | bytes 6291460 | tf_op jit(solution)/shard_map/while/body/eval_jaxpr/cond
  47.9 1.4 %copy-start.1 = (f32[2,8,256,128]{3,2,1,0:T(8,128)}, f32[2,8,256,128]{3,2,1,0:T(8,128)S(1)}, u32[]{:S(2)}) copy-start(f32[2,8,256,128]{3,2,1,0:T(8,128)S(1)} %multiply_add_fusion) | copy-start | bytes 6291460 | tf_op jit(solution)/shard_map/while/body/eval_jaxpr/cond
  56.7 3.5 %copy-start = (f32[2,8,256,128]{3,2,1,0:T(8,128)S(1)}, f32[2,8,256,128]{3,2,1,0:T(8,128)}, u32[]{:S(2)}) copy-start(f32[2,8,256,128]{3,2,1,0:T(8,128)} %get-tuple-element.237) | copy-start | bytes 6291460 | tf_op jit(solution)/shard_map/while/body/eval_jaxpr/cond
  63.6 1.4 %copy-start.1 = (f32[2,8,256,128]{3,2,1,0:T(8,128)}, f32[2,8,256,128]{3,2,1,0:T(8,128)S(1)}, u32[]{:S(2)}) copy-start(f32[2,8,256,128]{3,2,1,0:T(8,128)S(1)} %multiply_add_fusion) | copy-start | bytes 6291460 | tf_op jit(solution)/shard_map/while/body/eval_jaxpr/cond
